TPU v7x, 32 devices: a whole 2x2x4 slice. The times are simulated.
32 devices in a mesh: blk: 32 (over z, y, x, core).
Axes of the slice: x: 2, y: 2, z: 4, core: 2. Of those that a mesh axis runs over, the one named last changes fastest.
Arguments:
- node_latent: bfloat16 [131072, 128], P('blk'), may hold values from -16 to 16
- edge_latent: bfloat16 [786432, 128], P('blk'), may hold values from -6 to 6
- edge_ends: int32 [2, 786432], P(None, 'blk'), may hold values from 0 to 5631, as said below
- edge_owned: int32 [786432], P('blk'), may hold values from 0 to 1, as said below
- send_index: int32 [32, 6, 256], P('blk'), may hold values from 0 to 4095, as said below
- edge_w1: bfloat16 [2, 384, 128], replicated, may hold values from -0.3125 to 0.3125
- edge_b1: float32 [2, 128], replicated, may hold values from -3 to 3
- edge_w2: bfloat16 [2, 128, 128], replicated, may hold values from -0.5 to 0.5
- edge_gain: float32 [2, 128], replicated, may hold values from 0.5 to 1.5
- edge_shift: float32 [2, 128], replicated, may hold values from -2 to 2
- node_w1: bfloat16 [2, 256, 128], replicated, may hold values from -0.375 to 0.375
- node_b1: float32 [2, 128], replicated, may hold values from -3 to 3
- node_w2: bfloat16 [2, 128, 128], replicated, may hold values from -0.5 to 0.5
- node_gain: float32 [2, 128], replicated, may hold values from 0.5 to 1.5
- node_shift: float32 [2, 128], replicated, may hold values from -2 to 2
Outputs:
- node_out: bfloat16 [131072, 128], P('blk')
- edge_out: bfloat16 [786432, 128], P('blk')
Inputs may be any that keep to these rules, and one draw needn't show every extreme that they name: edge_ends[0] holds each slot's sender, edge_ends[1] its receiver, as entries of the block's extended node list. Slot s of a block lies in tile t = s // 128; each of its ends is either an own node from (t // 6) * 128 to (t // 6 + 1) * 128 - 1 or a halo entry from 4096 + (t % 6) * 256 to 4096 + (t % 6 + 1) * 256 - 1; at most one end of a slot is a halo entry. `edge_owned`: in each block the slots with 1 come first; every block has at least 15360 of them. send_index[b, k] lists 256 distinct nodes of block b.
All inputs are finite; a program needn't handle non-finite values.
Results may differ from a plain program's by a relative error of at most 0.0085.
Values may be sent and summed in bfloat16 or wider, within the bound.
A program may use at most 128 MiB of HBM per device.

v0:
```python
import jax
import jax.numpy as jnp
from jax import lax
from jax.sharding import PartitionSpec as P

LAYERS = 2
FACES = 6
GX = 4
GY = 4


def passed_along(block, axis, distance):
    devices = range(lax.axis_size(axis))
    route = [((i - distance) % len(devices), i) for i in devices]
    return lax.ppermute(block, axis, route)


def row_norm(mixed):
    centre = mixed - jnp.mean(mixed, axis=1, keepdims=True)
    spread = jnp.mean(centre * centre, axis=1, keepdims=True)
    return centre * lax.rsqrt(spread + 1e-05)


def one_hots(ends, own_rows, halo_rows, tile_rows, dtype):
    groups = own_rows // tile_rows
    index = ends.reshape(groups, FACES, tile_rows)
    own_local = index - (jnp.arange(groups, dtype=jnp.int32) * tile_rows)[:, None, None]
    halo_local = index - own_rows - (jnp.arange(FACES, dtype=jnp.int32) * halo_rows)[None, :, None]
    own_hot = (own_local[..., None] == jnp.arange(tile_rows, dtype=jnp.int32)).astype(dtype)
    halo_hot = (halo_local[..., None] == jnp.arange(halo_rows, dtype=jnp.int32)).astype(dtype)
    return (own_hot, halo_hot)


def select_rows(hots, own_table, halo_table):
    own_hot, halo_hot = hots
    groups, faces, tile_rows, _ = own_hot.shape
    columns = own_table.shape[1]
    own_view = own_table.reshape(groups, tile_rows, columns)
    halo_view = halo_table.reshape(faces, halo_hot.shape[3], columns)
    picked = jnp.einsum(
        "bken,bnc->bkec", own_hot, own_view, preferred_element_type=jnp.float32, precision=None
    )
    picked = picked + jnp.einsum(
        "bkeh,khc->bkec", halo_hot, halo_view, preferred_element_type=jnp.float32, precision=None
    )
    return picked.reshape(groups * faces * tile_rows, columns)


def per_device(
    node_latent,
    edge_latent,
    edge_ends,
    edge_owned,
    send_index,
    edge_w1,
    edge_b1,
    edge_w2,
    edge_gain,
    edge_shift,
    node_w1,
    node_b1,
    node_w2,
    node_gain,
    node_shift,
):
    width = node_latent.shape[1]
    own_rows = node_latent.shape[0]
    halo_rows = send_index.shape[2]
    tile_rows = min(128, own_rows)
    groups = own_rows // tile_rows
    offsets = (1, -1, GX, -GX, GX * GY, -GX * GY)
    face_rows = send_index[0]
    flat_faces = face_rows.reshape(-1)
    owned = edge_owned.astype(jnp.float32)[:, None]
    total_nodes = own_rows * lax.axis_size("blk")
    recv_hots = one_hots(edge_ends[1], own_rows, halo_rows, tile_rows, jnp.bfloat16)
    latents = node_latent
    edge_state = edge_latent
    for layer_id in range(LAYERS):
        w_first = edge_w1[layer_id]
        outgoing = latents[face_rows]
        arrived = [
            passed_along(outgoing[face_id], "blk", offsets[face_id]) for face_id in range(FACES)
        ]
        halo_table = jnp.concatenate(arrived, axis=0)
        send_hots = one_hots(edge_ends[0], own_rows, halo_rows, tile_rows, jnp.bfloat16)
        from_send = select_rows(send_hots, latents, halo_table).astype(jnp.bfloat16)
        from_recv = select_rows(recv_hots, latents, halo_table).astype(jnp.bfloat16)
        joined = jnp.concatenate([edge_state, from_send, from_recv], axis=1)
        before = jnp.dot(joined, w_first, preferred_element_type=jnp.float32)
        hidden = jax.nn.relu(before + edge_b1[layer_id]).astype(jnp.bfloat16)
        mixed = jnp.dot(hidden, edge_w2[layer_id], preferred_element_type=jnp.float32)
        normed = edge_gain[layer_id] * row_norm(mixed) + edge_shift[layer_id]
        edges_new = (edge_state.astype(jnp.float32) + owned * normed).astype(jnp.bfloat16)
        message = (
            (owned * edges_new.astype(jnp.float32))
            .astype(jnp.bfloat16)
            .reshape(groups, FACES, tile_rows, width)
        )
        own_sums = jnp.einsum(
            "bken,bkec->bnc", recv_hots[0], message, preferred_element_type=jnp.float32
        ).reshape(own_rows, width)
        halo_sums = jnp.einsum(
            "bkeh,bkec->khc", recv_hots[1], message, preferred_element_type=jnp.float32
        )
        returned = [
            passed_along(halo_sums[face_id].astype(jnp.bfloat16), "blk", -offsets[face_id]).astype(
                jnp.float32
            )
            for face_id in range(FACES)
        ]
        node_sums = own_sums.at[flat_faces].add(jnp.concatenate(returned, axis=0))
        aggregate = node_sums.astype(jnp.bfloat16)
        node_in = jnp.concatenate([latents, aggregate], axis=1)
        node_hidden = jax.nn.relu(
            jnp.dot(node_in, node_w1[layer_id], preferred_element_type=jnp.float32)
            + node_b1[layer_id]
        ).astype(jnp.bfloat16)
        update = jnp.dot(node_hidden, node_w2[layer_id], preferred_element_type=jnp.float32)
        sums, squares = lax.psum((jnp.sum(update, axis=0), jnp.sum(update * update, axis=0)), "blk")
        centre_mean = sums / total_nodes
        variance = jnp.maximum(squares / total_nodes - centre_mean * centre_mean, 0.0)
        deviation = update - centre_mean
        latents = (
            latents.astype(jnp.float32)
            + node_gain[layer_id] * deviation * lax.rsqrt(variance + 1e-05)
            + node_shift[layer_id]
        ).astype(jnp.bfloat16)
        edge_state = edges_new
    return (latents, edge_state)


def solution(mesh):
    placed = (
        P("blk", None),
        P("blk", None),
        P(None, "blk"),
        P("blk"),
        P("blk", None, None),
        P(),
        P(),
        P(),
        P(),
        P(),
        P(),
        P(),
        P(),
        P(),
        P(),
    )
    return jax.shard_map(
        per_device,
        mesh=mesh,
        in_specs=placed,
        out_specs=(P("blk", None), P("blk", None)),
        check_vma=False,
    )
```

profile of v0, /device:TPU:10, one launch (start us, length us, event | category | flops | bytes accessed | tf_op | source)
XLA Modules:
  0.0 363.1 jit_solution(16261037858530044124)
XLA Ops:
  1.5 4.0 %gather_fusion = bf16[1536,128]{1,0:T(8,128)(2,1)S(1)} fusion(bf16[4096,128]{1,0:T(8,128)(2,1)} %param.15, s32[2048]{0:T(1024)S(1)} %pad_clamp_fusion), kind=kCustom, calls=%fused_computation | custom fusion | bytes 792576 | tf_op jit(solution)/shard_map/gather | solution.py:81
  5.5 2.7 collective-permute-start.5
  8.5 1.4 collective-permute-start.3
  11.3 1.2 slice_bitcast_fusion.13
  13.4 1.5 slice_reduce_fusion
  15.2 7.9 %fusion.33 = f32[32,6,128,128]{3,2,1,0:T(8,128)S(1)} fusion(bf16[32,128,128,1]{2,1,3,0:T(8,128)(2,1)S(1)} %bitcast.163, s32[32,6,128]{2,1,0:T(8,128)S(1)} %get-tuple-element.44), kind=kOutput, calls=%fused_computation.52 | convolution fusion | flops 808452096 | bytes 13729792 | tf_op jit(solution)/shard_map/bken,bnc->bkec/dot_general | solution.py:40
  23.1 3.4 fusion.37
  27.7 2.3 collective-permute-start.1
  30.0 1.9 collective-permute-done.1
  32.0 8.3 %fusion.29 = bf16[32,6,128,128]{3,2,1,0:T(8,128)(2,1)} fusion(f32[32,6,128,128]{3,2,1,0:T(8,128)S(1)} %fusion.33, bf16[6,256,128,1]{2,1,0,3:T(8,128)(2,1)S(1)} %bitcast.172, s32[32,6,128]{2,0,1:T(8,128)S(1)} %copy.29), kind=kOutput, calls=%fused_computation.43 | convolution fusion | flops 1623195648 | bytes 19365888 | tf_op jit(solution)/shard_map/bkeh,khc->bkec/dot_general | solution.py:43
  40.3 8.8 %fusion.28 = bf16[32,6,128,128]{3,2,1,0:T(8,128)(2,1)} fusion(f32[32,6,128,128]{3,2,1,0:T(8,128)S(1)} %fusion.37, bf16[6,256,128,1]{2,1,0,3:T(8,128)(2,1)S(1)} %bitcast.173, s32[32,6,128]{2,0,1:T(8,128)S(1)} %copy.32), kind=kOutput, calls=%fused_computation.41 | convolution fusion | flops 1623195648 | bytes 19365888 | tf_op jit(solution)/shard_map/bkeh,khc->bkec/dot_general | solution.py:43
  49.1 14.5 %fusion.139 = (f32[24576]{0:T(1024)S(1)}, f32[24576,128]{1,0:T(8,128)}) fusion(bf16[2,128,128]{2,1,0:T(8,128)(2,1)S(1)} %copy-done.15, bf16[24576,128]{1,0:T(8,128)(2,1)} %bitcast.179, bf16[24576,128]{1,0:T(8,128)(2,1)} %bitcast.178, bf16[24576,128]{1,0:T(8,128)(2,1)} %param.16, f32[128]{0:T(128)S(1)} %get-tuple-element.55, ...), kind=kOutput, calls=%fused_computation.195 | convolution fusion | flops 3290406912 | bytes 31687168 | tf_op jit(solution)/shard_map/dot_general | solution.py:92
  63.6 10.2 %multiply_reduce_fusion.1 = f32[24576]{0:T(1024)S(1)} fusion(f32[24576,128]{1,0:T(8,128)} %get-tuple-element.63, f32[24576]{0:T(1024)S(1)} %broadcast_multiply_fusion.1), kind=kLoop, calls=%fused_computation.47 | loop fusion | flops 9412608 | bytes 12779520 | tf_op jit(solution)/shard_map/reduce_sum | solution.py:20
  73.9 22.2 %fusion.24 = (bf16[24576,128]{1,0:T(8,128)(2,1)S(1)}, bf16[24576,128]{1,0:T(8,128)(2,1)}) fusion(f32[24576]{0:T(1024)S(1)} %convert_element_type.146, f32[128]{0:T(128)S(1)} %get-tuple-element.69, f32[24576]{0:T(1024)S(1)} %add_rsqrt_fusion.1, f32[24576,128]{1,0:T(8,128)S(1)} %copy-done.1, f32[24576]{0:T(1024)S(1)} %broadcast_multiply_fusion.1, ...), kind=kLoop, calls=%fused_computation.34 | loop fusion | flops 34603008 | bytes 31753216 | tf_op jit(solution)/shard_map/convert_element_type | solution.py:97
  96.1 3.7 %fusion.85 = bf16[6,256,128]{2,1,0:T(8,128)(2,1)S(1)} fusion(bf16[32,6,128,128]{3,2,1,0:T(8,128)(2,1)S(1)} %bitcast.167, s32[32,6,128]{2,0,1:T(8,128)S(1)} %copy.32), kind=kOutput, calls=%fused_computation.89 | convolution fusion | flops 1617100800 | bytes 6782976 | tf_op jit(solution)/shard_map/bkeh,bkec->khc/dot_general | solution.py:103
  99.9 2.0 collective-permute-start.6
  101.9 3.6 %fusion.36 = f32[32,128,128,1]{2,1,3,0:T(8,128)} fusion(bf16[32,6,128,128]{3,2,1,0:T(8,128)(2,1)S(1)} %bitcast.168, s32[32,6,128]{2,1,0:T(8,128)S(1)} %get-tuple-element.43), kind=kOutput, calls=%fused_computation.56 | convolution fusion | flops 808452096 | bytes 8486912 | tf_op jit(solution)/shard_map/bken,bkec->bnc/dot_general | solution.py:100
  105.6 2.6 collective-permute-start.11
  108.5 3.9 %collective-permute-start.9 = (bf16[256,128]{1,0:T(8,128)(2,1)S(1)}, bf16[256,128]{1,0:T(8,128)(2,1)S(1)}, u32[]{:S(2)}, u32[]{:S(2)}) collective-permute-start(bf16[256,128]{1,0:T(8,128)(2,1)S(1)} %get-tuple-element.30), channel_id=1, source_target_pairs={{28,0},{29,1},{30,2},{31,3},{0,4},{1,5},{2,6},{3,7},{4,8},{5,9},{6... | collective-permute-start | bytes 196616 | tf_op jit(solution)/shard_map/ppermute | solution.py:15
  112.4 1.4 collective-permute-start.7
  113.8 2.3 collective-permute-done.7
  117.2 10.8 %scatter_custom_fusion = f32[4096,128]{1,0:T(8,128)} fusion(f32[4096,128]{1,0:T(8,128)} %bitcast.170, s32[1536]{0:T(1024)S(1)} %fusion.121, bf16[1536,128]{1,0:T(8,128)(2,1)S(1)} %constant_dynamic-update-slice_fusion.6), kind=kCustom, calls=%fused_computation.96 | custom fusion | flops 393216 | bytes 2490368 | tf_op jit(solution)/shard_map/scatter-add | solution.py:112
  128.0 1.7 convert_element_type.162
  129.7 2.6 fusion.135
  132.3 52.1 %all-reduce.1 = (f32[128]{0:T(128)S(1)}, f32[128]{0:T(128)S(1)}) all-reduce(f32[128]{0:T(128)S(1)} %get-tuple-element.5, f32[128]{0:T(128)S(1)} %get-tuple-element.4), channel_id=1, replica_groups=mesh['blk'=32] {'blk'}, use_global_device_ids=true, to_apply=%region_6.7 | all-reduce | flops 256 | bytes 2048 | tf_op jit(solution)/shard_map/psum | solution.py:120
  184.3 2.1 add_convert_fusion.2
  186.4 3.2 gather_fusion.1
  189.7 7.9 %fusion.32 = f32[32,6,128,128]{3,2,1,0:T(8,128)S(1)} fusion(bf16[32,128,128,1]{2,1,3,0:T(8,128)(2,1)S(1)} %bitcast.161, s32[32,6,128]{2,1,0:T(8,128)S(1)} %get-tuple-element.44), kind=kOutput, calls=%fused_computation.51 | convolution fusion | flops 808452096 | bytes 13729792 | tf_op jit(solution)/shard_map/bken,bnc->bkec/dot_general | solution.py:40
  197.6 3.4 fusion.35
  201.1 2.9 collective-permute-start.16
  204.0 2.3 collective-permute-start.14
  206.8 1.9 collective-permute-done.13
  208.7 1.2 collective-permute-done.14
  210.4 8.2 %fusion.27 = bf16[32,6,128,128]{3,2,1,0:T(8,128)(2,1)} fusion(f32[32,6,128,128]{3,2,1,0:T(8,128)S(1)} %fusion.32, bf16[6,256,128,1]{2,1,0,3:T(8,128)(2,1)S(1)} %bitcast.174, s32[32,6,128]{2,0,1:T(8,128)S(1)} %copy.29), kind=kOutput, calls=%fused_computation.39 | convolution fusion | flops 1623195648 | bytes 19365888 | tf_op jit(solution)/shard_map/bkeh,khc->bkec/dot_general | solution.py:43
  218.6 8.8 %fusion.26 = bf16[32,6,128,128]{3,2,1,0:T(8,128)(2,1)} fusion(f32[32,6,128,128]{3,2,1,0:T(8,128)S(1)} %fusion.35, bf16[6,256,128,1]{2,1,0,3:T(8,128)(2,1)S(1)} %bitcast.175, s32[32,6,128]{2,0,1:T(8,128)S(1)} %copy.32), kind=kOutput, calls=%fused_computation.37 | convolution fusion | flops 1623195648 | bytes 19365888 | tf_op jit(solution)/shard_map/bkeh,khc->bkec/dot_general | solution.py:43
  227.4 14.5 %fusion.148 = (f32[24576]{0:T(1024)S(1)}, f32[24576,128]{1,0:T(8,128)}) fusion(bf16[2,128,128]{2,1,0:T(8,128)(2,1)S(1)} %copy-done.15, bf16[24576,128]{1,0:T(8,128)(2,1)} %bitcast.177, bf16[24576,128]{1,0:T(8,128)(2,1)} %bitcast.176, bf16[24576,128]{1,0:T(8,128)(2,1)} %get-tuple-element.15, f32[128]{0:T(128)S(1)} %get-tuple-element.54, ...), kind=kOutput, calls=%fused_computation.196 | convolution fusion | flops 3290406912 | bytes 31687168 | tf_op jit(solution)/shard_map/dot_general | solution.py:92
  241.9 10.6 %multiply_reduce_fusion = f32[24576]{0:T(1024)S(1)} fusion(f32[24576,128]{1,0:T(8,128)} %get-tuple-element.66, f32[24576]{0:T(1024)S(1)} %broadcast_multiply_fusion), kind=kLoop, calls=%fused_computation.45 | loop fusion | flops 9412608 | bytes 12779520 | tf_op jit(solution)/shard_map/reduce_sum | solution.py:20
  252.6 22.2 %multiply_convert_fusion = (bf16[24576,128]{1,0:T(8,128)(2,1)S(1)}, bf16[24576,128]{1,0:T(8,128)(2,1)}) fusion(f32[24576]{0:T(1024)S(1)} %convert_element_type.146, f32[128]{0:T(128)S(1)} %copy-done.7, f32[24576]{0:T(1024)S(1)} %add_rsqrt_fusion, f32[24576,128]{1,0:T(8,128)S(1)} %copy-done, f32[24576]{0:T(1024)S(1)} %broadcast_multiply_fusion, ...), kind=kLoop, calls=%fused_computation.44 | loop fusion | flops 34603008 | bytes 31753216 | tf_op jit(solution)/shard_map/convert_element_type | solution.py:97
  274.8 3.7 %fusion.82 = bf16[6,256,128]{2,1,0:T(8,128)(2,1)S(1)} fusion(bf16[32,6,128,128]{3,2,1,0:T(8,128)(2,1)S(1)} %bitcast.165, s32[32,6,128]{2,0,1:T(8,128)S(1)} %copy.32), kind=kOutput, calls=%fused_computation.88 | convolution fusion | flops 1617100800 | bytes 6782976 | tf_op jit(solution)/shard_map/bkeh,bkec->khc/dot_general | solution.py:103
  279.1 3.7 %fusion.34 = f32[32,128,128,1]{2,1,3,0:T(8,128)} fusion(bf16[32,6,128,128]{3,2,1,0:T(8,128)(2,1)S(1)} %bitcast.166, s32[32,6,128]{2,1,0:T(8,128)S(1)} %get-tuple-element.43), kind=kOutput, calls=%fused_computation.54 | convolution fusion | flops 808452096 | bytes 8486912 | tf_op jit(solution)/shard_map/bken,bkec->bnc/dot_general | solution.py:100
  282.8 2.4 collective-permute-start.23
  285.7 2.3 collective-permute-start.21
  289.1 3.2 collective-permute-done.19
  293.6 10.8 %scatter_custom_fusion.1 = f32[4096,128]{1,0:T(8,128)} fusion(f32[4096,128]{1,0:T(8,128)} %bitcast.169, s32[1536]{0:T(1024)S(1)} %fusion.121, bf16[1536,128]{1,0:T(8,128)(2,1)S(1)} %constant_dynamic-update-slice_fusion.18), kind=kCustom, calls=%fused_computation.94 | custom fusion | flops 393216 | bytes 2490368 | tf_op jit(solution)/shard_map/scatter-add | solution.py:112
  304.4 1.7 convert_element_type.180
  306.1 2.6 fusion.134
  308.6 51.0 %all-reduce = (f32[128]{0:T(128)S(1)}, f32[128]{0:T(128)S(1)}) all-reduce(f32[128]{0:T(128)S(1)} %get-tuple-element.3, f32[128]{0:T(128)S(1)} %get-tuple-element.2), channel_id=1, replica_groups=mesh['blk'=32] {'blk'}, use_global_device_ids=true, to_apply=%region_13.14 | all-reduce | flops 256 | bytes 2048 | tf_op jit(solution)/shard_map/psum | solution.py:120
  359.7 3.0 add_convert_fusion.1
  (115 shorter events, 10.9 us)
Async XLA Ops:
  0.6 14.5 %copy-start.2 = (bf16[4096,128]{1,0:T(8,128)(2,1)S(1)}, bf16[4096,128]{1,0:T(8,128)(2,1)}, u32[]{:S(2)}) copy-start(bf16[4096,128]{1,0:T(8,128)(2,1)} %param.15) | copy-start | bytes 3145732
  5.5 26.5 %collective-permute-start.5 = (bf16[256,128]{1,0:T(8,128)(2,1)S(1)}, bf16[256,128]{1,0:T(8,128)(2,1)S(1)}, u32[]{:S(2)}, u32[]{:S(2)}) collective-permute-start(bf16[256,128]{1,0:T(8,128)(2,1)S(1)} %get-tuple-element.34), channel_id=1, source_target_pairs={{16,0},{17,1},{18,2},{19,3},{20,4},{21,5},{22,6},{23,7},{24,8},{25... | collective-permute-start | bytes 196616 | tf_op jit(solution)/shard_map/ppermute | solution.py:15
  8.2 23.8 %collective-permute-start.4 = (bf16[256,128]{1,0:T(8,128)(2,1)S(1)}, bf16[256,128]{1,0:T(8,128)(2,1)S(1)}, u32[]{:S(2)}, u32[]{:S(2)}) collective-permute-start(bf16[256,128]{1,0:T(8,128)(2,1)S(1)} %get-tuple-element.35), channel_id=1, source_target_pairs={{16,0},{17,1},{18,2},{19,3},{20,4},{21,5},{22,6},{23,7},{24,8},{25... | collective-permute-start | bytes 196616 | tf_op jit(solution)/shard_map/ppermute | solution.py:15
  8.5 23.4 %collective-permute-start.3 = (bf16[256,128]{1,0:T(8,128)(2,1)S(1)}, bf16[256,128]{1,0:T(8,128)(2,1)S(1)}, u32[]{:S(2)}, u32[]{:S(2)}) collective-permute-start(bf16[256,128]{1,0:T(8,128)(2,1)S(1)} %get-tuple-element.36), channel_id=1, source_target_pairs={{4,0},{5,1},{6,2},{7,3},{8,4},{9,5},{10,6},{11,7},{12,8},{13,9},{1... | collective-permute-start | bytes 196616 | tf_op jit(solution)/shard_map/ppermute | solution.py:15
  9.9 22.0 %collective-permute-start.2 = (bf16[256,128]{1,0:T(8,128)(2,1)S(1)}, bf16[256,128]{1,0:T(8,128)(2,1)S(1)}, u32[]{:S(2)}, u32[]{:S(2)}) collective-permute-start(bf16[256,128]{1,0:T(8,128)(2,1)S(1)} %get-tuple-element.37), channel_id=1, source_target_pairs={{28,0},{29,1},{30,2},{31,3},{0,4},{1,5},{2,6},{3,7},{4,8},{5,9},{6... | collective-permute-start | bytes 196616 | tf_op jit(solution)/shard_map/ppermute | solution.py:15
  10.5 17.2 %collective-permute-start = (bf16[256,128]{1,0:T(8,128)(2,1)S(1)}, bf16[256,128]{1,0:T(8,128)(2,1)S(1)}, u32[]{:S(2)}, u32[]{:S(2)}) collective-permute-start(bf16[256,128]{1,0:T(8,128)(2,1)S(1)} %get-tuple-element.39), channel_id=1, source_target_pairs={{31,0},{0,1},{1,2},{2,3},{3,4},{4,5},{5,6},{6,7},{7,8},{8,9},{9,10... | collective-permute-start | bytes 196616 | tf_op jit(solution)/shard_map/ppermute | solution.py:15
  23.0 3.5 copy-start.8
  23.1 3.5 copy-start.9
  23.1 4.0 %copy-start.10 = (f32[2,128]{1,0:T(2,128)S(1)}, f32[2,128]{1,0:T(2,128)}, u32[]{:S(2)}) copy-start(f32[2,128]{1,0:T(2,128)} %param.29) | copy-start | bytes 3076
  23.1 4.0 %copy-start.11 = (f32[2,128]{1,0:T(2,128)S(1)}, f32[2,128]{1,0:T(2,128)}, u32[]{:S(2)}) copy-start(f32[2,128]{1,0:T(2,128)} %param.28) | copy-start | bytes 3076
  23.1 4.6 %copy-start.3 = (s32[1,6,256]{2,0,1:T(1,128)S(1)}, s32[1,6,256]{2,0,1:T(1,128)}, u32[]{:S(2)}) copy-start(s32[1,6,256]{2,0,1:T(1,128)} %param.19) | copy-start | bytes 18436
  27.7 4.2 %collective-permute-start.1 = (bf16[256,128]{1,0:T(8,128)(2,1)S(1)}, bf16[256,128]{1,0:T(8,128)(2,1)S(1)}, u32[]{:S(2)}, u32[]{:S(2)}) collective-permute-start(bf16[256,128]{1,0:T(8,128)(2,1)S(1)} %get-tuple-element.38), channel_id=1, source_target_pairs={{1,0},{2,1},{3,2},{4,3},{5,4},{6,5},{7,6},{8,7},{9,8},{10,9},{11,1... | collective-permute-start | bytes 196616 | tf_op jit(solution)/shard_map/ppermute | solution.py:15
  40.3 8.8 %copy-start.13 = (bf16[2,384,128]{2,1,0:T(8,128)(2,1)S(1)}, bf16[2,384,128]{2,1,0:T(8,128)(2,1)}, u32[]{:S(2)}) copy-start(bf16[2,384,128]{2,1,0:T(8,128)(2,1)} %param.20) | copy-start | bytes 589828
  40.3 8.8 %copy-start.15 = (bf16[2,128,128]{2,1,0:T(8,128)(2,1)S(1)}, bf16[2,128,128]{2,1,0:T(8,128)(2,1)}, u32[]{:S(2)}) copy-start(bf16[2,128,128]{2,1,0:T(8,128)(2,1)} %param.22) | copy-start | bytes 196612
  63.6 10.3 %copy-start.1 = (f32[24576,128]{1,0:T(8,128)S(1)}, f32[24576,128]{1,0:T(8,128)}, u32[]{:S(2)}) copy-start(f32[24576,128]{1,0:T(8,128)} %get-tuple-element.63) | copy-start | bytes 37748740
  99.9 12.5 %collective-permute-start.6 = (bf16[256,128]{1,0:T(8,128)(2,1)S(1)}, bf16[256,128]{1,0:T(8,128)(2,1)S(1)}, u32[]{:S(2)}, u32[]{:S(2)}) collective-permute-start(bf16[256,128]{1,0:T(8,128)(2,1)S(1)} %get-tuple-element.33), channel_id=1, source_target_pairs={{1,0},{2,1},{3,2},{4,3},{5,4},{6,5},{7,6},{8,7},{9,8},{10,9},{11,1... | collective-permute-start | bytes 196616 | tf_op jit(solution)/shard_map/ppermute | solution.py:15
  105.6 24.1 %copy-start.14 = (bf16[2,256,128]{2,1,0:T(8,128)(2,1)S(1)}, bf16[2,256,128]{2,1,0:T(8,128)(2,1)}, u32[]{:S(2)}) copy-start(bf16[2,256,128]{2,1,0:T(8,128)(2,1)} %param.25) | copy-start | bytes 393220
  105.6 24.1 %copy-start.16 = (bf16[2,128,128]{2,1,0:T(8,128)(2,1)S(1)}, bf16[2,128,128]{2,1,0:T(8,128)(2,1)}, u32[]{:S(2)}) copy-start(bf16[2,128,128]{2,1,0:T(8,128)(2,1)} %param.27) | copy-start | bytes 196612
  105.6 11.6 %collective-permute-start.11 = (bf16[256,128]{1,0:T(8,128)(2,1)S(1)}, bf16[256,128]{1,0:T(8,128)(2,1)S(1)}, u32[]{:S(2)}, u32[]{:S(2)}) collective-permute-start(bf16[256,128]{1,0:T(8,128)(2,1)S(1)} %get-tuple-element.28), channel_id=1, source_target_pairs={{16,0},{17,1},{18,2},{19,3},{20,4},{21,5},{22,6},{23,7},{24,8},{25... | collective-permute-start | bytes 196616 | tf_op jit(solution)/shard_map/ppermute | solution.py:15
  108.1 9.0 %collective-permute-start.10 = (bf16[256,128]{1,0:T(8,128)(2,1)S(1)}, bf16[256,128]{1,0:T(8,128)(2,1)S(1)}, u32[]{:S(2)}, u32[]{:S(2)}) collective-permute-start(bf16[256,128]{1,0:T(8,128)(2,1)S(1)} %get-tuple-element.29), channel_id=1, source_target_pairs={{16,0},{17,1},{18,2},{19,3},{20,4},{21,5},{22,6},{23,7},{24,8},{25... | collective-permute-start | bytes 196616 | tf_op jit(solution)/shard_map/ppermute | solution.py:15
  108.5 8.6 %collective-permute-start.9 = (bf16[256,128]{1,0:T(8,128)(2,1)S(1)}, bf16[256,128]{1,0:T(8,128)(2,1)S(1)}, u32[]{:S(2)}, u32[]{:S(2)}) collective-permute-start(bf16[256,128]{1,0:T(8,128)(2,1)S(1)} %get-tuple-element.30), channel_id=1, source_target_pairs={{28,0},{29,1},{30,2},{31,3},{0,4},{1,5},{2,6},{3,7},{4,8},{5,9},{6... | collective-permute-start | bytes 196616 | tf_op jit(solution)/shard_map/ppermute | solution.py:15
  112.4 4.7 %collective-permute-start.8 = (bf16[256,128]{1,0:T(8,128)(2,1)S(1)}, bf16[256,128]{1,0:T(8,128)(2,1)S(1)}, u32[]{:S(2)}, u32[]{:S(2)}) collective-permute-start(bf16[256,128]{1,0:T(8,128)(2,1)S(1)} %get-tuple-element.31), channel_id=1, source_target_pairs={{4,0},{5,1},{6,2},{7,3},{8,4},{9,5},{10,6},{11,7},{12,8},{13,9},{1... | collective-permute-start | bytes 196616 | tf_op jit(solution)/shard_map/ppermute | solution.py:15
  112.4 3.7 %collective-permute-start.7 = (bf16[256,128]{1,0:T(8,128)(2,1)S(1)}, bf16[256,128]{1,0:T(8,128)(2,1)S(1)}, u32[]{:S(2)}, u32[]{:S(2)}) collective-permute-start(bf16[256,128]{1,0:T(8,128)(2,1)S(1)} %get-tuple-element.32), channel_id=1, source_target_pairs={{31,0},{0,1},{1,2},{2,3},{3,4},{4,5},{5,6},{6,7},{7,8},{8,9},{9,10... | collective-permute-start | bytes 196616 | tf_op jit(solution)/shard_map/ppermute | solution.py:15
  189.7 16.6 %collective-permute-start.12 = (bf16[256,128]{1,0:T(8,128)(2,1)S(1)}, bf16[256,128]{1,0:T(8,128)(2,1)S(1)}, u32[]{:S(2)}, u32[]{:S(2)}) collective-permute-start(bf16[256,128]{1,0:T(8,128)(2,1)S(1)} %get-tuple-element.27), channel_id=1, source_target_pairs={{31,0},{0,1},{1,2},{2,3},{3,4},{4,5},{5,6},{6,7},{7,8},{8,9},{9,10... | collective-permute-start | bytes 196616 | tf_op jit(solution)/shard_map/ppermute | solution.py:15
  201.0 9.3 %collective-permute-start.17 = (bf16[256,128]{1,0:T(8,128)(2,1)S(1)}, bf16[256,128]{1,0:T(8,128)(2,1)S(1)}, u32[]{:S(2)}, u32[]{:S(2)}) collective-permute-start(bf16[256,128]{1,0:T(8,128)(2,1)S(1)} %get-tuple-element.22), channel_id=1, source_target_pairs={{16,0},{17,1},{18,2},{19,3},{20,4},{21,5},{22,6},{23,7},{24,8},{25... | collective-permute-start | bytes 196616 | tf_op jit(solution)/shard_map/ppermute | solution.py:15
  201.1 9.2 %collective-permute-start.16 = (bf16[256,128]{1,0:T(8,128)(2,1)S(1)}, bf16[256,128]{1,0:T(8,128)(2,1)S(1)}, u32[]{:S(2)}, u32[]{:S(2)}) collective-permute-start(bf16[256,128]{1,0:T(8,128)(2,1)S(1)} %get-tuple-element.23), channel_id=1, source_target_pairs={{16,0},{17,1},{18,2},{19,3},{20,4},{21,5},{22,6},{23,7},{24,8},{25... | collective-permute-start | bytes 196616 | tf_op jit(solution)/shard_map/ppermute | solution.py:15
  204.0 6.3 %collective-permute-start.15 = (bf16[256,128]{1,0:T(8,128)(2,1)S(1)}, bf16[256,128]{1,0:T(8,128)(2,1)S(1)}, u32[]{:S(2)}, u32[]{:S(2)}) collective-permute-start(bf16[256,128]{1,0:T(8,128)(2,1)S(1)} %get-tuple-element.24), channel_id=1, source_target_pairs={{4,0},{5,1},{6,2},{7,3},{8,4},{9,5},{10,6},{11,7},{12,8},{13,9},{1... | collective-permute-start | bytes 196616 | tf_op jit(solution)/shard_map/ppermute | solution.py:15
  204.0 5.9 %collective-permute-start.14 = (bf16[256,128]{1,0:T(8,128)(2,1)S(1)}, bf16[256,128]{1,0:T(8,128)(2,1)S(1)}, u32[]{:S(2)}, u32[]{:S(2)}) collective-permute-start(bf16[256,128]{1,0:T(8,128)(2,1)S(1)} %get-tuple-element.25), channel_id=1, source_target_pairs={{28,0},{29,1},{30,2},{31,3},{0,4},{1,5},{2,6},{3,7},{4,8},{5,9},{6... | collective-permute-start | bytes 196616 | tf_op jit(solution)/shard_map/ppermute | solution.py:15
  206.3 2.4 collective-permute-start.13
  241.9 10.7 %copy-start = (f32[24576,128]{1,0:T(8,128)S(1)}, f32[24576,128]{1,0:T(8,128)}, u32[]{:S(2)}) copy-start(f32[24576,128]{1,0:T(8,128)} %get-tuple-element.66) | copy-start | bytes 37748740
  241.9 10.7 %copy-start.6 = (f32[128]{0:T(128)S(1)}, f32[128]{0:T(128)}, u32[]{:S(2)}) copy-start(f32[128]{0:T(128)} %get-tuple-element.52) | copy-start | bytes 1540
  241.9 10.7 %copy-start.7 = (f32[128]{0:T(128)S(1)}, f32[128]{0:T(128)}, u32[]{:S(2)}) copy-start(f32[128]{0:T(128)} %get-tuple-element.68) | copy-start | bytes 1540
  278.6 10.1 %collective-permute-start.18 = (bf16[256,128]{1,0:T(8,128)(2,1)S(1)}, bf16[256,128]{1,0:T(8,128)(2,1)S(1)}, u32[]{:S(2)}, u32[]{:S(2)}) collective-permute-start(bf16[256,128]{1,0:T(8,128)(2,1)S(1)} %get-tuple-element.21), channel_id=1, source_target_pairs={{1,0},{2,1},{3,2},{4,3},{5,4},{6,5},{7,6},{8,7},{9,8},{10,9},{11,1... | collective-permute-start | bytes 196616 | tf_op jit(solution)/shard_map/ppermute | solution.py:15
  282.8 23.3 %copy-start.12 = (f32[128]{0:T(128)S(1)}, f32[128]{0:T(128)}, u32[]{:S(2)}) copy-start(f32[128]{0:T(128)} %get-tuple-element.50) | copy-start | bytes 1540
  282.8 10.7 %collective-permute-start.23 = (bf16[256,128]{1,0:T(8,128)(2,1)S(1)}, bf16[256,128]{1,0:T(8,128)(2,1)S(1)}, u32[]{:S(2)}, u32[]{:S(2)}) collective-permute-start(bf16[256,128]{1,0:T(8,128)(2,1)S(1)} %get-tuple-element.16), channel_id=1, source_target_pairs={{16,0},{17,1},{18,2},{19,3},{20,4},{21,5},{22,6},{23,7},{24,8},{25... | collective-permute-start | bytes 196616 | tf_op jit(solution)/shard_map/ppermute | solution.py:15
  285.2 8.3 %collective-permute-start.22 = (bf16[256,128]{1,0:T(8,128)(2,1)S(1)}, bf16[256,128]{1,0:T(8,128)(2,1)S(1)}, u32[]{:S(2)}, u32[]{:S(2)}) collective-permute-start(bf16[256,128]{1,0:T(8,128)(2,1)S(1)} %get-tuple-element.17), channel_id=1, source_target_pairs={{16,0},{17,1},{18,2},{19,3},{20,4},{21,5},{22,6},{23,7},{24,8},{25... | collective-permute-start | bytes 196616 | tf_op jit(solution)/shard_map/ppermute | solution.py:15
  285.7 7.7 %collective-permute-start.21 = (bf16[256,128]{1,0:T(8,128)(2,1)S(1)}, bf16[256,128]{1,0:T(8,128)(2,1)S(1)}, u32[]{:S(2)}, u32[]{:S(2)}) collective-permute-start(bf16[256,128]{1,0:T(8,128)(2,1)S(1)} %get-tuple-element.18), channel_id=1, source_target_pairs={{28,0},{29,1},{30,2},{31,3},{0,4},{1,5},{2,6},{3,7},{4,8},{5,9},{6... | collective-permute-start | bytes 196616 | tf_op jit(solution)/shard_map/ppermute | solution.py:15
  288.0 5.4 %collective-permute-start.20 = (bf16[256,128]{1,0:T(8,128)(2,1)S(1)}, bf16[256,128]{1,0:T(8,128)(2,1)S(1)}, u32[]{:S(2)}, u32[]{:S(2)}) collective-permute-start(bf16[256,128]{1,0:T(8,128)(2,1)S(1)} %get-tuple-element.19), channel_id=1, source_target_pairs={{4,0},{5,1},{6,2},{7,3},{8,4},{9,5},{10,6},{11,7},{12,8},{13,9},{1... | collective-permute-start | bytes 196616 | tf_op jit(solution)/shard_map/ppermute | solution.py:15
  288.6 3.7 %collective-permute-start.19 = (bf16[256,128]{1,0:T(8,128)(2,1)S(1)}, bf16[256,128]{1,0:T(8,128)(2,1)S(1)}, u32[]{:S(2)}, u32[]{:S(2)}) collective-permute-start(bf16[256,128]{1,0:T(8,128)(2,1)S(1)} %get-tuple-element.20), channel_id=1, source_target_pairs={{31,0},{0,1},{1,2},{2,3},{3,4},{4,5},{5,6},{6,7},{7,8},{8,9},{9,10... | collective-permute-start | bytes 196616 | tf_op jit(solution)/shard_map/ppermute | solution.py:15
  293.5 66.1 %copy-start.4 = (f32[128]{0:T(128)S(1)}, f32[128]{0:T(128)}, u32[]{:S(2)}) copy-start(f32[128]{0:T(128)} %get-tuple-element.48) | copy-start | bytes 1540
  293.5 66.1 %copy-start.5 = (f32[128]{0:T(128)S(1)}, f32[128]{0:T(128)}, u32[]{:S(2)}) copy-start(f32[128]{0:T(128)} %get-tuple-element.71) | copy-start | bytes 1540
where the time goes:
time: 368 us; the launch traced here: 363 us
  matrix products  106 us (29%)
  blocking collectives  103 us (28%)
  other arithmetic  97.3 us (26%)
  starting transfers between devices  30.2 us (8%)
  waiting for transfers between devices  13 us (4%)
  local copies, waits for them, and re-layouts  12.4 us (3%)
    psum x2, blocking collectives, per_device(): lax.psum((jnp.sum(update, axis=0), jnp.sum(update * update, axis=0)), 'blk')  103 us
    convert_element_type x2, other arithmetic, per_device(): message = (owned * edges_new.astype(jnp.float32)).astype(jnp.bfloat16).re...  44.4 us
    dot_general x4, matrix products, select_rows(): jnp.einsum('bkeh,khc->bkec', halo_hot, halo_view, preferred_element_type=...  34.1 us
    ppermute x24, starting transfers between devices, passed_along(): return lax.ppermute(block, axis, route)  30.2 us
    dot_general x2, matrix products, per_device(): jnp.dot(hidden, edge_w2[layer_id], preferred_element_type=jnp.float32)  29 us
    dot_general x4, matrix products, select_rows(): jnp.einsum('bken,bnc->bkec', own_hot, own_view, preferred_element_type=jn...  22.6 us
    scatter-add x2, other arithmetic, per_device(): node_sums = own_sums.at[flat_faces].add(jnp.concatenate(returned, axis=0))  21.6 us
    reduce_sum x2, other arithmetic, row_norm(): spread = jnp.mean(centre * centre, axis=1, keepdims=True)  20.9 us
  transfers between devices with their start and end apart: 24, of which 8 were waited for; matrix products, arithmetic and copies ran while one was open for 10% of the time, Pallas kernels for 0%

commit v1 on v0

v1 whole, which is shorter than its diff:
```python
import functools

import jax
import jax.numpy as jnp
from jax import lax
from jax.experimental import pallas as pl
from jax.experimental.pallas import tpu as pltpu
from jax.sharding import PartitionSpec as P

LAYERS = 2
FACES = 6
GX = 4
GY = 4
MESH = pl.DeviceIdType.MESH
VMEM = pltpu.VMEM
F32 = jnp.float32
BF16 = jnp.bfloat16


def dot(a, b):
    return jnp.dot(a, b, preferred_element_type=F32)


def hot(mask):
    return jnp.where(mask, 1.0, 0.0).astype(BF16)


def iota(shape, axis):
    return lax.broadcasted_iota(jnp.int32, shape, axis)


def face_target(me, face, n, sign):
    step = jnp.where(face < 2, 1, jnp.where(face < 4, GX, GX * GY))
    step = jnp.where(face % 2 == 0, step, -step) * sign
    return lax.rem(me + step + n * GX * GY, n)


def edge_kernel(layer, own_rows, halo_rows, e_ref, ends_ref, owned_ref, tab_ref, phalo_ref,
                w1_ref, b1_ref, w2_ref, gain_ref, shift_ref,
                out_ref, own_ref, halo_ref, acc, bd1, bd2):
    step = pl.program_id(0)
    steps = pl.num_programs(0)
    tile = ends_ref.shape[3]
    width = e_ref.shape[1]
    rows = FACES * tile

    @pl.when(step == 0)
    def _():
        acc[...] = jnp.zeros_like(acc)
        bd1[...] = jnp.zeros_like(bd1)
        bd2[...] = jnp.zeros_like(bd2)
        for i in range(2):
            bd1[i * width:(i + 1) * width, i * width:(i + 1) * width] = w1_ref[layer, 0:width, :]
            bd2[i * width:(i + 1) * width, i * width:(i + 1) * width] = w2_ref[layer]

    per_step = ends_ref.shape[1]
    face = iota((FACES, tile), 0)
    lane = iota((rows, tile), 1)
    bias = b1_ref[layer:layer + 1, :]
    gain = gain_ref[layer:layer + 1, :]
    shift = shift_ref[layer:layer + 1, :]
    for pair in range(per_step // 2):
        hots, tables, recv_rows, halo_recv, flags_r, flags_o, pre = [], [], [], [], [], [], []
        halo_hots = []
        for i in range(2):
            local = pair * 2 + i
            group = step * per_step + local
            s = ends_ref[0, local]
            r = ends_ref[1, local]
            ok = owned_ref[local] > 0
            s_halo = s >= own_rows
            r_halo = r >= own_rows
            so = jnp.where(ok & ~s_halo, s - group * tile, 255)
            ro = jnp.where(ok & ~r_halo, r - group * tile, 255)
            base = own_rows + face * halo_rows
            hs = jnp.where(s_halo, s - base, jnp.where(r_halo, r - base, 511))
            hc = jnp.where(ok, hs, 511)
            recv_rows.append(ro)
            halo_recv.append(jnp.where(ok & r_halo, r - base, 511))
            code = (so | (ro << 8) | (hc << 16) | jnp.where(r_halo, 1 << 25, 0)
                    | jnp.where(ok, 1 << 26, 0))
            cols = jnp.concatenate(
                [jnp.broadcast_to(code[k:k + 1, :], (tile, tile)).T for k in range(FACES)], axis=0)
            sr = jnp.concatenate(
                [hot((cols & 255) == lane), hot(((cols >> 8) & 255) == lane)], axis=1)
            hcol = (cols >> 16) & 511
            halo_hots.append(jnp.concatenate([hot(hcol == lane + j * tile)
                                              for j in range(halo_rows // tile)], axis=1))
            flags_r.append((cols & (1 << 25)) != 0)
            flags_o.append((cols & (1 << 26)) != 0)
            pre.append(dot(sr, tab_ref[local]))
        from_halo = [[], []]
        for k in range(FACES):
            at = slice(k * tile, (k + 1) * tile)
            both = dot(jnp.concatenate([halo_hots[0][at], halo_hots[1][at]], axis=0), phalo_ref[k])
            for i in range(2):
                part = both[i * tile:(i + 1) * tile]
                from_halo[i].append(jnp.where(flags_r[i][at], part[:, width:], part[:, :width]))
        edges = [e_ref[(pair * 2 + i) * rows:(pair * 2 + i + 1) * rows, :] for i in range(2)]
        from_e = dot(jnp.concatenate(edges, axis=1), bd1[...])
        hidden = []
        for i in range(2):
            before = from_e[:, i * width:(i + 1) * width] + pre[i] + jnp.concatenate(from_halo[i], axis=0)
            hidden.append(jnp.maximum(before + bias, 0.0).astype(BF16))
        mixed2 = dot(jnp.concatenate(hidden, axis=1), bd2[...])
        fresh = []
        for i in range(2):
            mixed = mixed2[:, i * width:(i + 1) * width]
            centre = mixed - jnp.mean(mixed, axis=1, keepdims=True)
            spread = jnp.mean(centre * centre, axis=1, keepdims=True)
            normed = gain * (centre * lax.rsqrt(spread + 1e-05)) + shift
            new = (edges[i].astype(F32) + jnp.where(flags_o[i], normed, 0.0)).astype(BF16)
            out_ref[(pair * 2 + i) * rows:(pair * 2 + i + 1) * rows, :] = new
            fresh.append(new)
            node = iota((tile, tile), 0)
            hot_t = jnp.concatenate([hot(recv_rows[i][k:k + 1, :] == node) for k in range(FACES)], axis=1)
            own_ref[(pair * 2 + i) * tile:(pair * 2 + i + 1) * tile, :] = dot(hot_t, new)
        node = iota((halo_rows, tile), 0)
        for k in range(FACES):
            at = slice(k * tile, (k + 1) * tile)
            hot_t = jnp.concatenate([hot(halo_recv[i][k:k + 1, :] == node) for i in range(2)], axis=1)
            acc[k] += dot(hot_t, jnp.concatenate([fresh[0][at], fresh[1][at]], axis=0))

    @pl.when(step == steps - 1)
    def _():
        halo_ref[...] = acc[...].astype(BF16)


def edge_layer(layer, e, ends, owned, tab, phalo, w1, b1, w2, gain, shift, own_rows, halo_rows):
    groups, tile = ends.shape[1], ends.shape[3]
    width = e.shape[1]
    per = 4 if groups % 4 == 0 else 2
    rows = FACES * tile
    whole = lambda a: pl.BlockSpec(a.shape, lambda i: (0,) * a.ndim)
    return pl.pallas_call(
        functools.partial(edge_kernel, layer, own_rows, halo_rows),
        grid=(groups // per,),
        in_specs=[
            pl.BlockSpec((per * rows, width), lambda i: (i, 0)),
            pl.BlockSpec((2, per, FACES, tile), lambda i: (0, i, 0, 0)),
            pl.BlockSpec((per, FACES, tile), lambda i: (i, 0, 0)),
            pl.BlockSpec((per, 2 * tile, width), lambda i: (i, 0, 0)),
            whole(phalo), whole(w1), whole(b1), whole(w2), whole(gain), whole(shift),
        ],
        out_specs=[
            pl.BlockSpec((per * rows, width), lambda i: (i, 0)),
            pl.BlockSpec((per * tile, width), lambda i: (i, 0)),
            pl.BlockSpec((FACES, halo_rows, width), lambda i: (0, 0, 0)),
        ],
        out_shape=[
            jax.ShapeDtypeStruct(e.shape, BF16),
            jax.ShapeDtypeStruct((own_rows, width), F32),
            jax.ShapeDtypeStruct((FACES, halo_rows, width), BF16),
        ],
        scratch_shapes=[
            VMEM((FACES, halo_rows, width), F32),
            VMEM((2 * width, 2 * width), BF16),
            VMEM((2 * width, 2 * width), BF16),
        ],
        compiler_params=pltpu.CompilerParams(dimension_semantics=("arbitrary",)),
    )(e, ends, owned, tab, phalo, w1, b1, w2, gain, shift)


def first_weights(w1_ref, layer, width):
    return jnp.concatenate(
        [w1_ref[layer, width:2 * width, :], w1_ref[layer, 2 * width:3 * width, :]], axis=1)


def exchange_latents(me, n, layer, h_ref, send_ref, w1_ref, tab_ref, phalo_ref, stage, landed, ssem, rsem):
    own_rows, width = h_ref.shape
    halo_rows = send_ref.shape[1]
    tile = 128
    chunk = min(1024, own_rows)
    weights = first_weights(w1_ref, layer, width)

    def copy(k):
        return pltpu.make_async_remote_copy(
            src_ref=stage.at[k], dst_ref=landed.at[k], send_sem=ssem.at[k], recv_sem=rsem.at[k],
            device_id=(face_target(me, k, n, 1),), device_id_type=MESH)

    @pl.loop(0, FACES)
    def _(k):
        row = send_ref[pl.ds(k, 1), :]
        cols = jnp.concatenate(
            [jnp.broadcast_to(row[:, j * tile:(j + 1) * tile], (tile, tile)).T
             for j in range(halo_rows // tile)], axis=0)
        lane = iota(cols.shape, 1)
        total = None
        for c in range(own_rows // chunk):
            one = jnp.concatenate(
                [hot(cols == lane + (c * chunk + j * tile)) for j in range(chunk // tile)], axis=1)
            part = dot(one, h_ref[c * chunk:(c + 1) * chunk, :])
            total = part if total is None else total + part
        stage[pl.ds(k, 1)] = total.astype(BF16)[None]
        copy(k).start()

    @pl.loop(0, tab_ref.shape[0])
    def _(g):
        both = dot(h_ref[pl.ds(pl.multiple_of(g * tile, tile), tile), :], weights).astype(BF16)
        tab_ref[pl.ds(g, 1)] = jnp.concatenate([both[:, :width], both[:, width:]], axis=0)[None]

    @pl.loop(0, FACES)
    def _(k):
        copy(k).wait()
        phalo_ref[pl.ds(k, 1)] = dot(landed[k], weights).astype(BF16)[None]


def first_kernel(n, h_ref, send_ref, w1_ref, tab_ref, phalo_ref, stage, landed, ssem, rsem):
    me = lax.axis_index("blk")
    barrier = pltpu.get_barrier_semaphore()
    for k in range(FACES):
        pl.semaphore_signal(barrier, inc=1, device_id=(face_target(me, k, n, 1),), device_id_type=MESH)
    pl.semaphore_wait(barrier, FACES)
    exchange_latents(me, n, 0, h_ref, send_ref, w1_ref, tab_ref, phalo_ref, stage, landed, ssem, rsem)


def node_kernel(n, layer, last, h_ref, own_ref, halo_ref, send_ref, ew1_ref, w1_ref, b1_ref, w2_ref,
                gain_ref, shift_ref, *rest):
    if last:
        out_ref, returned, update, mine, stats, ssem, rsem, tsem, usem = rest
    else:
        (out_ref, tab_ref, phalo_ref, returned, update, mine, stats, ssem, rsem, tsem, usem,
         stage, landed, ssem2, rsem2) = rest
    me = lax.axis_index("blk")
    own_rows, width = h_ref.shape
    halo_rows = send_ref.shape[1]
    barrier = pltpu.get_barrier_semaphore()

    @pl.loop(1, n)
    def _(j):
        pl.semaphore_signal(barrier, inc=1, device_id=(lax.rem(me + j, n),), device_id_type=MESH)

    pl.semaphore_wait(barrier, n - 1)

    def copy(k):
        return pltpu.make_async_remote_copy(
            src_ref=halo_ref.at[k], dst_ref=returned.at[k], send_sem=ssem.at[k], recv_sem=rsem.at[k],
            device_id=(face_target(me, k, n, -1),), device_id_type=MESH)

    for k in range(FACES):
        copy(k).start()
    for k in range(FACES):
        copy(k).wait()
    back = returned[...].reshape(FACES * halo_rows, width)
    chunk = min(512, own_rows)

    def body(c, carry):
        sums, squares = carry
        first = pl.multiple_of(c * chunk, chunk)
        at = pl.ds(first, chunk)
        node = iota((chunk, halo_rows), 0) + first
        one = jnp.concatenate([hot(send_ref[k:k + 1, :] == node) for k in range(FACES)], axis=1)
        agg = (own_ref[at, :] + dot(one, back)).astype(BF16)
        joined = jnp.concatenate([h_ref[at, :], agg], axis=1)
        hidden = jnp.maximum(dot(joined, w1_ref[layer]) + b1_ref[layer:layer + 1, :], 0.0).astype(BF16)
        upd = dot(hidden, w2_ref[layer])
        update[at, :] = upd
        return (sums + jnp.sum(upd, axis=0, keepdims=True),
                squares + jnp.sum(upd * upd, axis=0, keepdims=True))

    zero = jnp.zeros((1, width), F32)
    sums, squares = lax.fori_loop(0, own_rows // chunk, body, (zero, zero))
    packed = jnp.concatenate([sums, squares, jnp.zeros((6, width), F32)], axis=0)
    mine[...] = packed
    stats[pl.ds(me, 1)] = packed[None]

    def share(j):
        return pltpu.make_async_remote_copy(
            src_ref=mine, dst_ref=stats.at[me], send_sem=tsem.at[j], recv_sem=usem.at[j],
            device_id=(lax.rem(me + j, n),), device_id_type=MESH)

    @pl.loop(1, n)
    def _(j):
        share(j).start()

    @pl.loop(1, n)
    def _(j):
        share(j).wait()

    total = jnp.sum(stats[...], axis=0)
    count = own_rows * n
    mean = total[0:1] / count
    variance = jnp.maximum(total[1:2] / count - mean * mean, 0.0)
    scale = gain_ref[layer:layer + 1, :] * lax.rsqrt(variance + 1e-05)
    shift = shift_ref[layer:layer + 1, :]

    @pl.loop(0, own_rows // chunk)
    def _(c):
        at = pl.ds(pl.multiple_of(c * chunk, chunk), chunk)
        out_ref[at, :] = (h_ref[at, :].astype(F32) + scale * (update[at, :] - mean) + shift).astype(BF16)

    if not last:
        exchange_latents(me, n, layer + 1, out_ref, send_ref, ew1_ref, tab_ref, phalo_ref,
                         stage, landed, ssem2, rsem2)


def per_device(n, node_latent, edge_latent, edge_ends, edge_owned, send_index, edge_w1, edge_b1, edge_w2,
               edge_gain, edge_shift, node_w1, node_b1, node_w2, node_gain, node_shift):
    own_rows, width = node_latent.shape
    halo_rows = send_index.shape[2]
    tile = 128
    groups = own_rows // tile
    ends = edge_ends.reshape(2, groups, FACES, tile)
    owned = edge_owned.reshape(groups, FACES, tile)
    send = send_index[0]
    tab_shape = jax.ShapeDtypeStruct((groups, 2 * tile, width), BF16)
    phalo_shape = jax.ShapeDtypeStruct((FACES, halo_rows, 2 * width), BF16)
    spec = pl.BlockSpec(memory_space=VMEM)
    faces = VMEM((FACES, halo_rows, width), BF16)
    sems = pltpu.SemaphoreType.DMA((FACES,))
    tab, phalo = pl.pallas_call(
        functools.partial(first_kernel, n),
        in_specs=[spec] * 3,
        out_specs=[spec] * 2,
        out_shape=[tab_shape, phalo_shape],
        scratch_shapes=[faces, faces, sems, sems],
        compiler_params=pltpu.CompilerParams(collective_id=0, has_side_effects=True),
    )(node_latent, send, edge_w1)
    latents, edges = node_latent, edge_latent
    for layer in range(LAYERS):
        edges, own_sums, halo_sums = edge_layer(
            layer, edges, ends, owned, tab, phalo, edge_w1, edge_b1, edge_w2, edge_gain, edge_shift,
            own_rows, halo_rows)
        last = layer == LAYERS - 1
        out = [jax.ShapeDtypeStruct((own_rows, width), BF16)]
        scratch = [faces, VMEM((own_rows, width), F32), VMEM((8, width), F32), VMEM((n, 8, width), F32),
                   sems, sems, pltpu.SemaphoreType.DMA((n,)), pltpu.SemaphoreType.DMA((n,))]
        if not last:
            out += [tab_shape, phalo_shape]
            scratch += [faces, faces, sems, sems]
        result = pl.pallas_call(
            functools.partial(node_kernel, n, layer, last),
            in_specs=[spec] * 10,
            out_specs=[spec] * len(out),
            out_shape=out,
            scratch_shapes=scratch,
            compiler_params=pltpu.CompilerParams(collective_id=1 + layer, has_side_effects=True),
        )(latents, own_sums, halo_sums, send, edge_w1, node_w1, node_b1, node_w2, node_gain, node_shift)
        latents = result[0]
        if not last:
            tab, phalo = result[1:]
    return (latents, edges)


def solution(mesh):
    row, rep = P("blk", None), P()
    return jax.shard_map(
        functools.partial(per_device, mesh.shape["blk"]),
        mesh=mesh,
        in_specs=(row, row, P(None, "blk"), P("blk"), P("blk", None, None)) + (rep,) * 10,
        out_specs=(row, row),
        check_vma=False,
    )
```

time: 368 us -> 157 us (0.43)
  Pallas kernels: 0 us -> 147 us
  matrix products: 106 us -> 0 us
  blocking collectives: 103 us -> 0 us
  other arithmetic: 97.3 us -> 0 us
  starting transfers between devices: 30.2 us -> 0 us
  waiting for transfers between devices: 13 us -> 0 us
  local copies, waits for them, and re-layouts: 12.4 us -> 6.89 us
    pallas_call x0 -> x5, Pallas kernels: none -> 147 us  [the longest x2 72.9 us: per_device(): pl.pallas_call(functools.partial(node_kernel, n, layer, last), in_specs=[...]
    dot_general x16 -> x0, matrix products: 106 us -> none  [the longest x4 34.1 us: select_rows(): jnp.einsum('bkeh,khc->bkec', halo_hot, halo_view, preferred_element_type=...]
    psum x2 -> x0, blocking collectives: 103 us -> none  [per_device(): lax.psum((jnp.sum(update, axis=0), jnp.sum(update * update, axis=0)), 'blk')]
    convert_element_type x7 -> x0, other arithmetic: 53.8 us -> none  [the longest x2 44.4 us: per_device(): message = (owned * edges_new.astype(jnp.float32)).astype(jnp.bfloat16).re...]
    ppermute x24 -> x0, starting transfers between devices: 30.2 us -> none  [passed_along(): return lax.ppermute(block, axis, route)]
    scatter-add x2 -> x0, other arithmetic: 21.6 us -> none  [per_device(): node_sums = own_sums.at[flat_faces].add(jnp.concatenate(returned, axis=0))]
    reduce_sum x2 -> x0, other arithmetic: 20.9 us -> none  [row_norm(): spread = jnp.mean(centre * centre, axis=1, keepdims=True)]
    ppermute x24 -> x0, waiting for transfers between devices: 13 us -> none  [passed_along(): return lax.ppermute(block, axis, route)]
  transfers between devices with their start and end apart: 24 -> 0, of which waited for: 8 -> 0; matrix products, arithmetic and copies ran while one was open for 10% -> 0% of each run, Pallas kernels for 0% -> 0%
where the time goes in v1:
time: 157 us; the launch traced here: 154 us
  Pallas kernels  147 us (94%)
  local copies, waits for them, and re-layouts  6.89 us (4%)
    pallas_call x2, Pallas kernels, per_device(): pl.pallas_call(functools.partial(node_kernel, n, layer, last), in_specs=[...  72.9 us
    pallas_call x2, Pallas kernels, edge_layer(): pl.pallas_call(functools.partial(edge_kernel, layer, own_rows, halo_rows)...  57.5 us
    pallas_call x1, Pallas kernels, per_device(): pl.pallas_call(functools.partial(first_kernel, n), in_specs=[spec] * 3, o...  16.4 us
    unnamed x2, local copies, waits for them, and re-layouts  3.55 us

profile of v1, /device:TPU:10, one launch (start us, length us, event | category | flops | bytes accessed | tf_op | source)
XLA Modules:
  0.0 154.4 jit_solution(15975910743057662023)
XLA Ops:
  0.6 1.3 copy.19
  1.9 1.6 %reshape.11.owned_ref = s32[32,6,128]{2,1,0:T(8,128)} reshape(s32[24576]{0:T(1024)} %param.18) | data formatting | bytes 196608 | tf_op jit(solution)/shard_map/reshape | solution.py:304
  3.5 1.8 %reshape.10.ends_ref = s32[2,32,6,128]{3,2,1,0:T(8,128)} reshape(s32[2,24576]{1,0:T(2,128)} %param.17) | data formatting | bytes 393216 | tf_op jit(solution)/shard_map/reshape | solution.py:303
  5.3 16.4 %shard_map.158 = (bf16[32,256,128]{2,1,0:T(8,128)(2,1)}, bf16[6,256,256]{2,1,0:T(8,128)(2,1)}) custom-call(bf16[4096,128]{1,0:T(8,128)(2,1)} %h_ref.3, s32[6,256]{1,0:T(8,128)} %bitcast.3, bf16[2,384,128]{2,1,0:T(8,128)(2,1)} %ew1_ref.3), custom_call_target="tpu_custom_call" | custom-call | tf_op jit(solution)/shard_map/pallas_call | solution.py:311
  21.7 28.8 %shard_map.159 = (bf16[24576,128]{1,0:T(8,128)(2,1)}, f32[4096,128]{1,0:T(8,128)}, bf16[6,256,128]{2,1,0:T(8,128)(2,1)}) custom-call(bf16[24576,128]{1,0:T(8,128)(2,1)} %e_ref.1, s32[2,32,6,128]{3,2,1,0:T(8,128)} %reshape.10.ends_ref, s32[32,6,128]{2,1,0:T(8,128)} %reshape.11.owned_ref, bf16[32,256,128]{2,1,0:T(8,128)(2,1)} %get-tuple-element.13.tab_ref, ...), custom_call_target="tpu_custom_call" | custom-call | tf_op jit(solution)/shard_map/pallas_call | solution.py:135
  50.5 42.4 %shard_map.160 = (bf16[4096,128]{1,0:T(8,128)(2,1)}, bf16[32,256,128]{2,1,0:T(8,128)(2,1)}, bf16[6,256,256]{2,1,0:T(8,128)(2,1)}) custom-call(bf16[4096,128]{1,0:T(8,128)(2,1)} %h_ref.3, f32[4096,128]{1,0:T(8,128)} %get-tuple-element.15.own_ref, bf16[6,256,128]{2,1,0:T(8,128)(2,1)} %get-tuple-element.16.halo_ref, s32[6,256]{1,0:T(8,128)} %bitcast.4, ...), custom_call_target="tpu_custom_call" | custom-call | tf_op jit(solution)/shard_map/pallas_call | solution.py:331
  92.8 28.8 %shard_map.161 = (bf16[24576,128]{1,0:T(8,128)(2,1)}, f32[4096,128]{1,0:T(8,128)}, bf16[6,256,128]{2,1,0:T(8,128)(2,1)}) custom-call(bf16[24576,128]{1,0:T(8,128)(2,1)} %get-tuple-element.18.e_ref, s32[2,32,6,128]{3,2,1,0:T(8,128)} %reshape.10.ends_ref, s32[32,6,128]{2,1,0:T(8,128)} %reshape.11.owned_ref, bf16[32,256,128]{2,1,0:T(8,128)(2,1)} %get-tuple-element.19.tab_ref, ...), custom_call_target="tpu_custom_call" | custom-call | tf_op jit(solution)/shard_map/pallas_call | solution.py:135
  121.6 30.5 %shard_map.162 = bf16[4096,128]{1,0:T(8,128)(2,1)} custom-call(bf16[4096,128]{1,0:T(8,128)(2,1)} %get-tuple-element.17.h_ref, f32[4096,128]{1,0:T(8,128)} %get-tuple-element.21.own_ref, bf16[6,256,128]{2,1,0:T(8,128)(2,1)} %get-tuple-element.22.halo_ref, s32[6,256]{1,0:T(8,128)} %bitcast.5, bf16[2,384,128]{2,1,0:T(8,128)(2,1)} %ew1_ref.3, ...), custom_call_target="tpu_custom_call" | custom-call | tf_op jit(solution)/shard_map/pallas_call | solution.py:331
  152.1 2.3 %copy.21 = bf16[4096,128]{1,0:T(8,128)(2,1)} copy(bf16[4096,128]{1,0:T(8,128)(2,1)} %shard_map.162) | data formatting | bytes 2097152
